TPU v7x, 512 devices: a whole 4x4x16 slice. The times are simulated.
512 devices in a mesh: bytes: 16 (over z), ctx: 8 (over x, core), tp: 4 (over y).
Axes of the slice: x: 4, y: 4, z: 16, core: 2. Of those that a mesh axis runs over, the one named last changes fastest.
Arguments:
- byte_values_sequence: int32 [24576], P(('bytes', 'ctx')), may hold values from 0 to 255
- offsets: int32 [24576], P(('bytes', 'ctx')), may hold values from 0 to 168, as said below
- byte_table: bfloat16 [256, 1024], replicated, may hold values from -6 to 6
- byte_query: bfloat16 [1024, 1024], P(None, 'tp'), may hold values from -1 to 1
- byte_key: bfloat16 [1024, 1024], P(None, 'tp'), may hold values from -16 to 16
- byte_value: bfloat16 [1024, 1024], P(None, 'tp'), may hold values from -0.1875 to 0.1875
- latent_query: bfloat16 [1024, 4096], P(None, ('ctx', 'tp')), may hold values from -1 to 1
- latent_key: bfloat16 [1024, 4096], P(None, ('ctx', 'tp')), may hold values from -16 to 16
- latent_value: bfloat16 [1024, 4096], P(None, ('ctx', 'tp')), may hold values from -0.1875 to 0.1875
- decode_weight: bfloat16 [4096, 1024], P(('ctx', 'tp')), may hold values from -1 to 1
Outputs:
- byte_output: bfloat16 [24576, 1024], P(('bytes', 'ctx'), 'tp')
Inputs may be any that keep to these rules, and one draw needn't show every extreme that they name: offsets[i] is 0 where a patch starts and offsets[i - 1] + 1 elsewhere; the first byte of every device's 192 bytes starts a patch; one device's bytes hold 24 to 72 patch starts and the bytes of the devices of one index of bytes hold at most 384; both most values are reached in every draw.
All inputs are finite; a program needn't handle non-finite values.
Results may differ from a plain program's by a relative error of at most 0.017.
Values may be sent and summed in bfloat16 or wider, within the bound.
No kernel may reach another device: no remote copies, remote signals or barrier semaphores. Data moves between devices by JAX's collectives and lax.ppermute only.
A program may use at most 64 MiB of HBM per device.

v0:
```python
import math
import jax
import jax.numpy as jnp
from jax import lax
from jax.sharding import PartitionSpec as P

DB = 1024
HEADS_B = 16
HEAD_L = 128
EPSILON = 1e-06
NEGATIVE = -1e30
FARAWAY = 1 << 30


def from_behind(value, axis, steps):
    count = lax.axis_size(axis)
    first, last = (max(0, -steps), min(count, count - steps))
    return lax.ppermute(value, axis, [(source, source + steps) for source in range(first, last)])


def copy_for_each(array, axis):
    copies = jnp.broadcast_to(array, (lax.axis_size(axis), *array.shape))
    return lax.all_to_all(copies, axis, split_axis=0, concat_axis=0, tiled=True)


def joined_along(tiles, dim):
    tiles = jnp.moveaxis(tiles, 0, dim)
    lengths = tiles.shape
    return tiles.reshape(*lengths[:dim], lengths[dim] * lengths[dim + 1], *lengths[dim + 2 :])


def collect(array, axis, dim):
    tiles = copy_for_each(array, axis)
    return joined_along(tiles, dim)


def sent_together(arrays, axis, dim, along):
    widths = [a.shape[along] for a in arrays]
    both = jnp.concatenate(arrays, axis=along)
    filled = lax.all_gather(both, axis, axis=dim, tiled=True)
    return tuple(jnp.split(filled, [sum(widths[:k]) for k in range(1, len(widths))], axis=along))


def cut_along(array, dim, count):
    before, after = (array.shape[:dim], array.shape[dim + 1 :])
    return jnp.moveaxis(array.reshape(*before, count, -1, *after), dim, 0)


def sent_and_summed(array, axis, dim):
    tiles = cut_along(array, dim, lax.axis_size(axis))
    arrived = lax.all_to_all(tiles, axis, split_axis=0, concat_axis=0, tiled=True)
    return arrived.astype(jnp.float32).sum(axis=0)


def norm_rows(values):
    values = values.astype(jnp.float32)
    return values * lax.rsqrt(jnp.mean(values * values, axis=-1, keepdims=True) + EPSILON)


def project(inputs, weight):
    return jnp.dot(inputs, weight, preferred_element_type=jnp.float32).astype(jnp.bfloat16)


def byte_project(byte_values_sequence, byte_table, weights):
    onehot = (
        byte_values_sequence[:, None] == jnp.arange(byte_table.shape[0], dtype=jnp.int32)[None, :]
    ).astype(jnp.bfloat16)
    embedded = jnp.dot(onehot, byte_table, preferred_element_type=jnp.float32)
    normed = norm_rows(embedded).astype(jnp.bfloat16)
    return tuple((project(normed, weight) for weight in weights))


def per_device(
    byte_values_sequence,
    offsets,
    byte_table,
    byte_query,
    byte_key,
    byte_value,
    latent_query,
    latent_key,
    latent_value,
    decode_weight,
):
    row_count = byte_values_sequence.shape[0]
    channels = byte_query.shape[1]
    heads_here = HEADS_B * channels // DB
    head_feature_width = channels // heads_here
    ctx_count = lax.axis_size("ctx")
    tp_count = lax.axis_size("tp")
    slot_cap = 3 * row_count // 8
    block_index = lax.axis_index(("bytes", "ctx"))
    byte_window_queries, byte_window_keys, values_b = byte_project(
        byte_values_sequence, byte_table, (byte_query, byte_key, byte_value)
    )
    earlier_ids = from_behind(byte_values_sequence, ("bytes", "ctx"), 1)
    keys_e, values_e = byte_project(earlier_ids, byte_table, (byte_key, byte_value))
    keys_w = jnp.concatenate([keys_e, byte_window_keys], axis=0).reshape(
        2 * row_count, heads_here, head_feature_width
    )
    values_w = jnp.concatenate([values_e, values_b], axis=0).reshape(
        2 * row_count, heads_here, head_feature_width
    )
    queries_w = byte_window_queries.reshape(row_count, heads_here, head_feature_width)
    query_pos = jnp.arange(row_count, dtype=jnp.int32)[:, None]
    key_pos = jnp.arange(2 * row_count, dtype=jnp.int32)[None, :]
    allowed_b = (
        (key_pos > query_pos)
        & (key_pos <= query_pos + row_count)
        & ((key_pos >= row_count) | (block_index > 0))
    )
    scores_b = jnp.einsum(
        "qhd,khd->hqk", queries_w, keys_w, preferred_element_type=jnp.float32
    ) / math.sqrt(head_feature_width)
    scores_b = jnp.where(allowed_b[None], scores_b, NEGATIVE)
    highest_b = jnp.max(scores_b, axis=-1, keepdims=True)
    weights_b = jnp.where(allowed_b[None], jnp.exp(scores_b - highest_b), 0.0)
    totals_b = jnp.sum(weights_b, axis=-1)
    blended = jnp.einsum(
        "hqk,khd->qhd", weights_b.astype(jnp.bfloat16), values_w, preferred_element_type=jnp.float32
    )
    encoded = (blended / totals_b.T[:, :, None]).reshape(row_count, channels).astype(jnp.bfloat16)
    starts = (offsets == 0).astype(jnp.int32)
    local_patch = jnp.cumsum(starts) - 1
    members = local_patch[None, :] == jnp.arange(slot_cap, dtype=jnp.int32)[:, None]
    patch_sums = jnp.dot(members.astype(jnp.bfloat16), encoded, preferred_element_type=jnp.float32)
    lengths = jnp.sum(members.astype(jnp.float32), axis=1)
    pooled = (patch_sums / jnp.maximum(lengths, 1.0)[:, None]).astype(jnp.bfloat16)
    gathered, patch_counts = (
        collect(pooled, ("ctx", "tp"), 0),
        collect(local_patch[-1:] + 1, ("ctx", "tp"), 0),
    )
    features = gathered.reshape(ctx_count, tp_count, slot_cap, channels).transpose(0, 2, 1, 3)
    features = features.reshape(ctx_count * slot_cap, tp_count * channels)
    patch_counts = patch_counts.reshape(ctx_count, tp_count)[:, 0]
    slot_ids = jnp.arange(slot_cap, dtype=jnp.int32)
    block_ids = lax.axis_index("bytes") * ctx_count + jnp.arange(ctx_count, dtype=jnp.int32)
    positions = jnp.where(
        slot_ids[None, :] < patch_counts[:, None],
        block_ids[:, None] * slot_cap + slot_ids[None, :],
        FARAWAY,
    ).reshape(-1)
    capacity = ctx_count * row_count // 4
    running = jnp.cumsum((positions < FARAWAY).astype(jnp.int32))
    targets = jnp.arange(capacity, dtype=jnp.int32)
    chosen = jnp.minimum(jnp.searchsorted(running, targets + 1), running.shape[0] - 1)
    features = features[chosen]
    positions = jnp.where(targets < running[-1], positions[chosen], FARAWAY)
    latent_in = norm_rows(features).astype(jnp.bfloat16)
    queries_l = project(latent_in, latent_query)
    keys_l = project(latent_in, latent_key)
    values_l = project(latent_in, latent_value)
    query_rows = queries_l.shape[0]
    heads_latent = queries_l.shape[1] // HEAD_L
    queries_h = queries_l.reshape(query_rows, heads_latent, HEAD_L)
    initial = (
        jnp.full((heads_latent, query_rows), NEGATIVE, jnp.float32),
        jnp.zeros((heads_latent, query_rows), jnp.float32),
        jnp.zeros((query_rows, heads_latent, HEAD_L), jnp.float32),
    )
    running_state = initial
    keys_p, values_p, places_p = (
        *sent_together((keys_l, values_l), "bytes", 0, 1),
        lax.all_gather(positions, "bytes", axis=0, tiled=True),
    )
    span_rows = keys_p.shape[0]

    def attend_block(state, step_index):
        highest, totals, accumulated = state
        keys_s = lax.dynamic_slice_in_dim(keys_p, step_index * query_rows, query_rows, 0).reshape(
            query_rows, heads_latent, HEAD_L
        )
        values_s = lax.dynamic_slice_in_dim(
            values_p, step_index * query_rows, query_rows, 0
        ).reshape(query_rows, heads_latent, HEAD_L)
        places = lax.dynamic_slice_in_dim(places_p, step_index * query_rows, query_rows, 0)
        attention_scores = jnp.einsum(
            "qhd,khd->hqk", queries_h, keys_s, preferred_element_type=jnp.float32
        ) / math.sqrt(HEAD_L)
        allowed = (places[None, :] <= positions[:, None])[None]
        highest_new = jnp.maximum(
            highest, jnp.max(jnp.where(allowed, attention_scores, NEGATIVE), axis=-1)
        )
        factor = jnp.exp(highest - highest_new)
        weights = jnp.where(allowed, jnp.exp(attention_scores - highest_new[:, :, None]), 0.0)
        totals = totals * factor + jnp.sum(weights, axis=-1)
        mixed_in = jnp.einsum(
            "hqk,khd->qhd",
            weights.astype(jnp.bfloat16),
            values_s,
            preferred_element_type=jnp.float32,
        )
        accumulated = accumulated * factor.T[:, :, None] + mixed_in
        return ((highest_new, totals, accumulated), None)

    running_state, _ = lax.scan(
        attend_block, running_state, jnp.arange(span_rows // query_rows, dtype=jnp.int32)
    )
    highest_l, totals_l, accumulated_l = running_state
    latent_out = (
        (accumulated_l / totals_l.T[:, :, None])
        .reshape(query_rows, heads_latent * HEAD_L)
        .astype(jnp.bfloat16)
    )
    shares = sent_and_summed(
        jnp.dot(latent_out, decode_weight, preferred_element_type=jnp.float32).astype(jnp.bfloat16),
        ("ctx", "tp"),
        0,
    )
    summed = collect(shares.astype(jnp.bfloat16), ("ctx", "tp"), 0).astype(shares.dtype)
    before = jnp.sum(
        jnp.where(jnp.arange(ctx_count, dtype=jnp.int32) < lax.axis_index("ctx"), patch_counts, 0)
    )
    mine = lax.dynamic_slice_in_dim(summed, lax.axis_index("tp") * channels, channels, 1)
    decoded_bytes = mine[before + local_patch]
    return (encoded.astype(jnp.float32) + decoded_bytes).astype(jnp.bfloat16)


def solution(mesh):
    return jax.shard_map(
        per_device,
        mesh=mesh,
        in_specs=(
            P(("bytes", "ctx")),
            P(("bytes", "ctx")),
            P(),
            P(None, "tp"),
            P(None, "tp"),
            P(None, "tp"),
            P(None, ("ctx", "tp")),
            P(None, ("ctx", "tp")),
            P(None, ("ctx", "tp")),
            P(("ctx", "tp"), None),
        ),
        out_specs=P(("bytes", "ctx"), "tp"),
        check_vma=False,
    )
```

profile of v0, /device:TPU:1, one launch (start us, length us, event | category | flops | bytes accessed | tf_op | source)
XLA Modules:
  0.0 257.1 jit_solution(15806933889242681807)
XLA Ops:
  6.5 4.6 %collective-permute-start = (s32[192]{0:T(256)}, s32[192]{0:T(256)S(1)}, u32[]{:S(2)}, u32[]{:S(2)}) collective-permute-start(s32[192]{0:T(256)} %param.14), channel_id=1, source_target_pairs={{0,4},{4,8},{8,12},{12,16},{16,20},{20,24},{24,28},{28,32},{32,36}... | collective-permute-start | bytes 2312 | tf_op jit(solution)/shard_map/ppermute | solution.py:18
  14.9 7.3 %all-to-all-start = ((s32[32,1,1]{2,1,0:T(1,128)}), s32[32,1,1]{2,1,0:T(1,128)S(1)}, u32[]{:S(2)}, u32[]{:S(2)}) async-start(s32[32,1,1]{2,1,0:T(1,128)} %broadcast_in_dim.111), calls=%async_computation | async-start | bytes 32768 | tf_op jit(solution)/shard_map/all_to_all | solution.py:23
  26.6 2.6 %all-to-all-done = s32[32,1,1]{2,1,0:T(1,128)S(1)} async-done(((s32[32,1,1]{2,1,0:T(1,128)}), s32[32,1,1]{2,1,0:T(1,128)S(1)}, u32[]{:S(2)}, u32[]{:S(2)}) %all-to-all-start) | async-done | bytes 160 | tf_op jit(solution)/shard_map/all_to_all | solution.py:23
  33.0 1.3 fusion.25
  37.2 4.8 %all-to-all-start.1 = ((bf16[32,72,256]{2,1,0:T(8,128)(2,1)}), bf16[32,72,256]{2,1,0:T(8,128)(2,1)S(1)}, u32[]{:S(2)}, u32[]{:S(2)}) async-start(bf16[32,72,256]{2,1,0:T(8,128)(2,1)} %broadcast_in_dim.118), calls=%async_computation.1 | async-start | bytes 2359296 | tf_op jit(solution)/shard_map/all_to_all | solution.py:23
  42.0 19.8 %while.39 = (s32[]{:T(128)}, u32[384]{0:T(512)S(1)}, u32[384]{0:T(512)S(1)}, s32[576]{0:T(1024)S(1)}, s32[]{:T(128)}, /*index=5*/s32[]{:T(128)}, s32[]{}) while((s32[]{:T(128)}, u32[384]{0:T(512)S(1)}, u32[384]{0:T(512)S(1)}, s32[576]{0:T(1024)S(1)}, s32[]{:T(128)}, /*index=5*/s32[]{:T(128)}, s32[]{}) %tuple.72), condition=%wide.region_10.11_spmd.clone, body=%wide.region_9.10_spmd.clone.sunk | while | flops 8324 | bytes 29541 | solution.py:146
  42.1 1.9 gather_fusion
  44.1 1.9 gather_fusion
  46.0 1.9 gather_fusion
  48.0 1.9 gather_fusion
  50.0 1.9 gather_fusion
  52.0 1.9 gather_fusion
  54.0 1.9 gather_fusion
  56.0 1.9 gather_fusion
  57.9 1.9 gather_fusion
  59.9 1.9 gather_fusion
  62.7 2.1 gather_fusion.2
  66.9 1.9 gather_fusion.1
  70.1 29.0 %all-gather = s32[16,1,384]{2,1,0:T(1,128)S(1)} all-gather(s32[1,1,384]{2,1,0:T(1,128)S(1)} %reshape.249), channel_id=1, replica_groups=mesh['bytes'=16,'ctx'=8,'tp'=4] {'bytes'}, dimensions={0}, use_global_device_ids=true | all-gather | bytes 26112 | tf_op jit(solution)/shard_map/all_gather | solution.py:164
  99.5 38.2 %all-gather.3.cloned.1.call-done = bf16[6144,256]{0,1:T(8,128)(2,1)} async-done(((bf16[384,256]{0,1:T(8,128)(2,1)}), bf16[6144,256]{0,1:T(8,128)(2,1)}) %all-gather.3.cloned.1.call-update) | async-done | bytes 3145744 | tf_op jit(solution)/shard_map/all_gather | solution.py:40
  137.7 3.3 %fusion.52 = (bf16[6144,128]{0,1:T(8,128)(2,1)S(1)}, bf16[6144,128]{0,1:T(8,128)(2,1)}) fusion(bf16[6144,256]{0,1:T(8,128)(2,1)} %all-gather.3.cloned.1.call-done), kind=kLoop, calls=%fused_computation.120 | loop fusion | bytes 6291456 | tf_op jit(solution)/shard_map/split | solution.py:41
  141.0 51.5 %while.40 = (s32[]{:T(128)}, f32[1,384]{1,0:T(1,128)S(1)}, f32[1,384]{1,0:T(1,128)S(1)}, f32[384,1,128]{0,2,1:T(8,128)S(1)}, s32[16]{0:T(128)S(1)}, /*index=5*/s...) while((s32[]{:T(128)}, f32[1,384]{1,0:T(1,128)S(1)}, ...), condition=%wide.region_15.16_spmd.clone, body=%wide.region_12.15_spmd.clone.sunk | while | flops 77416712 | bytes 2498263 | solution.py:196
  142.4 1.2 fusion.84
  145.7 1.2 fusion.84
  148.9 1.2 fusion.84
  174.6 1.2 fusion.84
  177.8 1.2 fusion.84
  181.1 1.2 fusion.84
  184.3 1.2 fusion.84
  193.1 33.0 %all_to_all.21 = bf16[32,12,1024]{2,1,0:T(8,128)(2,1)S(1)} all-to-all(bf16[32,12,1024]{2,1,0:T(8,128)(2,1)S(1)} %reshape.208), channel_id=1, replica_groups=mesh['bytes'=16,'ctx'=8,'tp'=4] {'ctx','tp'}, dimensions={0} | all-to-all | bytes 1572864 | tf_op jit(solution)/shard_map/all_to_all | solution.py:51
  227.4 4.8 %all-to-all-start.3 = ((bf16[32,12,1024]{2,1,0:T(8,128)(2,1)}), bf16[32,12,1024]{2,1,0:T(8,128)(2,1)S(1)}, u32[]{:S(2)}, u32[]{:S(2)}) async-start(bf16[32,12,1024]{2,1,0:T(8,128)(2,1)} %broadcast_in_dim.119), calls=%async_computation.3 | async-start | bytes 2097152 | tf_op jit(solution)/shard_map/all_to_all | solution.py:23
  233.6 14.9 %all-to-all-done.3 = bf16[32,12,1024]{2,1,0:T(8,128)(2,1)S(1)} async-done(((bf16[32,12,1024]{2,1,0:T(8,128)(2,1)}), bf16[32,12,1024]{2,1,0:T(8,128)(2,1)S(1)}, u32[]{:S(2)}, u32[]{:S(2)}) %all-to-all-start.3) | async-done | bytes 786464 | tf_op jit(solution)/shard_map/all_to_all | solution.py:23
  (300 shorter events, 55.1 us)
Async XLA Ops:
  6.5 15.8 %copy-start = (bf16[256,1024]{1,0:T(8,128)(2,1)S(1)}, bf16[256,1024]{1,0:T(8,128)(2,1)}, u32[]{:S(2)}) copy-start(bf16[256,1024]{1,0:T(8,128)(2,1)} %param.16) | copy-start | bytes 1572868
  6.5 24.7 %collective-permute-start = (s32[192]{0:T(256)}, s32[192]{0:T(256)S(1)}, u32[]{:S(2)}, u32[]{:S(2)}) collective-permute-start(s32[192]{0:T(256)} %param.14), channel_id=1, source_target_pairs={{0,4},{4,8},{8,12},{12,16},{16,20},{20,24},{24,28},{28,32},{32,36}... | collective-permute-start | bytes 2312 | tf_op jit(solution)/shard_map/ppermute | solution.py:18
  12.5 0.6 copy-start.13
  13.1 10.4 %copy-start.17 = (s32[192]{0:T(256)}, s32[192]{0:T(256)S(1)}, u32[]{:S(2)}) copy-start(s32[192]{0:T(256)S(1)} %slice_add_fusion) | copy-start | bytes 2308
  14.9 14.2 %all-to-all-start = ((s32[32,1,1]{2,1,0:T(1,128)}), s32[32,1,1]{2,1,0:T(1,128)S(1)}, u32[]{:S(2)}, u32[]{:S(2)}) async-start(s32[32,1,1]{2,1,0:T(1,128)} %broadcast_in_dim.111), calls=%async_computation | async-start | bytes 32768 | tf_op jit(solution)/shard_map/all_to_all | solution.py:23
  22.3 1.3 copy-start.1
  23.5 1.0 copy-start.4
  23.7 1.1 copy-start.2
  26.4 5.8 %copy-start.6 = (pred[192,384]{1,0:T(8,128)(4,1)}, pred[192,384]{1,0:T(8,128)(4,1)S(1)}, u32[]{:S(2)}) copy-start(pred[192,384]{1,0:T(8,128)(4,1)S(1)} %fusion.34) | copy-start | bytes 221188
  26.6 5.7 %copy-start.3 = (bf16[192,256]{0,1:T(8,128)(2,1)}, bf16[192,256]{0,1:T(8,128)(2,1)S(1)}, u32[]{:S(2)}) copy-start(bf16[192,256]{0,1:T(8,128)(2,1)S(1)} %copy.33) | copy-start | bytes 294916
  30.0 0.6 copy-start.15
  31.7 0.6 copy-start.11
  33.0 1.4 copy-start.12
  33.0 1.7 copy-start.5
  34.4 0.9 copy-start.7
  35.2 0.6 copy-start.18
  35.2 0.6 copy-start.22
  35.8 1.4 copy-start.9
  37.2 24.7 %all-to-all-start.1 = ((bf16[32,72,256]{2,1,0:T(8,128)(2,1)}), bf16[32,72,256]{2,1,0:T(8,128)(2,1)S(1)}, u32[]{:S(2)}, u32[]{:S(2)}) async-start(bf16[32,72,256]{2,1,0:T(8,128)(2,1)} %broadcast_in_dim.118), calls=%async_computation.1 | async-start | bytes 2359296 | tf_op jit(solution)/shard_map/all_to_all | solution.py:23
  42.0 95.8 %all-gather.3.cloned.1.call-start = ((), (), s32[]{:S(2)}) async-start(), calls=%async_computation.4 | async-start | bytes 3342336 | tf_op jit(solution)/shard_map/all_gather | solution.py:40
  62.7 2.3 copy-start.19
  64.7 1.0 copy-start.20
  66.9 32.2 %copy-start.21 = (bf16[1024,128]{1,0:T(8,128)(2,1)S(1)}, bf16[1024,128]{1,0:T(8,128)(2,1)}, u32[]{:S(2)}) copy-start(bf16[1024,128]{1,0:T(8,128)(2,1)} %param.20) | copy-start | bytes 786436
  141.0 51.5 %copy-start.8 = (bf16[128,1024]{1,0:T(8,128)(2,1)S(1)}, bf16[128,1024]{1,0:T(8,128)(2,1)}, u32[]{:S(2)}) copy-start(bf16[128,1024]{1,0:T(8,128)(2,1)} %param.23) | copy-start | bytes 786436
  227.4 4.8 %copy-start.16 = (s32[8]{0:T(128)S(1)}, s32[8]{0:T(128)}, u32[]{:S(2)}) copy-start(s32[8]{0:T(128)} %copy-done.15) | copy-start | bytes 100
  227.4 5.4 %copy-start.14 = (s32[256]{0:T(256)S(1)}, s32[256]{0:T(256)}, u32[]{:S(2)}) copy-start(s32[256]{0:T(256)} %copy-done.13) | copy-start | bytes 3076
  227.4 6.1 %copy-start.10 = (bf16[192,4,64]{0,2,1:T(8,128)(2,1)S(1)}, bf16[192,4,64]{0,2,1:T(8,128)(2,1)}, u32[]{:S(2)}) copy-start(bf16[192,4,64]{0,2,1:T(8,128)(2,1)} %copy-done.9) | copy-start | bytes 294916
  227.4 21.1 %all-to-all-start.3 = ((bf16[32,12,1024]{2,1,0:T(8,128)(2,1)}), bf16[32,12,1024]{2,1,0:T(8,128)(2,1)S(1)}, u32[]{:S(2)}, u32[]{:S(2)}) async-start(bf16[32,12,1024]{2,1,0:T(8,128)(2,1)} %broadcast_in_dim.119), calls=%async_computation.3 | async-start | bytes 2097152 | tf_op jit(solution)/shard_map/all_to_all | solution.py:23
Sparse Core Ops, SparseCore 0:
  67.0 70.6 all-gather.2
where the time goes:
time: 258 us; the launch traced here: 257 us
  blocking collectives  62 us (24%)
  waiting for transfers between devices  55.7 us (22%)
  local copies, waits for them, and re-layouts  47.7 us (18%)
  matrix products  32.5 us (13%)
  starting transfers between devices  21.5 us (8%)
  between operations  14.6 us (6%)
  loops' own time  12.5 us (5%)
  other arithmetic  10.6 us (4%)
    all_gather x1, waiting for transfers between devices, sent_together(): filled = lax.all_gather(both, axis, axis=dim, tiled=True)  38.2 us
    all_to_all x1, blocking collectives, sent_and_summed(): lax.all_to_all(tiles, axis, split_axis=0, concat_axis=0, tiled=True)  33 us
    all_gather x1, blocking collectives, per_device(): lax.all_gather(positions, 'bytes', axis=0, tiled=True)  29 us
    dot_general x16, matrix products, attend_block(): jnp.einsum('qhd,khd->hqk', queries_h, keys_s, preferred_element_type=jnp....  18.9 us
    gather x10, local copies, waits for them, and re-layouts, per_device(): jnp.searchsorted(running, targets + 1)  18.9 us
    all_to_all x3, waiting for transfers between devices, copy_for_each(): return lax.all_to_all(copies, axis, split_axis=0, concat_axis=0, tiled=True)  17.5 us
    all_to_all x3, starting transfers between devices, copy_for_each(): return lax.all_to_all(copies, axis, split_axis=0, concat_axis=0, tiled=True)  16.9 us
    another operation x1, loops' own time, per_device(): lax.scan(attend_block, running_state, jnp.arange(span_rows // query_rows,...  11.9 us
  transfers between devices with their start and end apart: 5, of which 3 were waited for; matrix products, arithmetic and copies ran while one was open for 12% of the time, Pallas kernels for 0%

commit v1 on v0

--- a/solution.py
+++ b/solution.py
@@ -3,6 +3,7 @@
 import jax.numpy as jnp
 from jax import lax
 from jax.sharding import PartitionSpec as P
+from jax.lax import all_to_all, axis_size
 
 DB = 1024
 HEADS_B = 16
@@ -82,6 +83,14 @@
     latent_value,
     decode_weight,
 ):
+
+    def choose_tracks_here(buf):
+        axis_id = "bytes"
+        w2 = axis_size(axis_id)
+        formed = jnp.concatenate(w2 * [buf], 0)
+        top = all_to_all(formed, axis_id, 0, 0, tiled=True)
+        return top
+
     row_count = byte_values_sequence.shape[0]
     channels = byte_query.shape[1]
     heads_here = HEADS_B * channels // DB
@@ -161,7 +170,7 @@
     running_state = initial
     keys_p, values_p, places_p = (
         *sent_together((keys_l, values_l), "bytes", 0, 1),
-        lax.all_gather(positions, "bytes", axis=0, tiled=True),
+        choose_tracks_here(positions),
     )
     span_rows = keys_p.shape[0]
 

time: 258 us -> 256 us (level)
  blocking collectives: 62 us -> 32.9 us
  starting transfers between devices: 21.5 us -> 36.1 us
  waiting for transfers between devices: 55.7 us -> 69.7 us
    all_gather x1 -> x0, blocking collectives: 29 us -> none  [per_device(): lax.all_gather(positions, 'bytes', axis=0, tiled=True)]
    all_to_all x0 -> x1, starting transfers between devices: none -> 14.5 us  [choose_tracks_here(): top = all_to_all(formed, axis_id, 0, 0, tiled=True)]
    all_gather x1, waiting for transfers between devices: 38.2 us -> 52.2 us  [sent_together(): filled = lax.all_gather(both, axis, axis=dim, tiled=True)]
  transfers between devices with their start and end apart: 5 -> 6, of which waited for: 3 -> 3; matrix products, arithmetic and copies ran while one was open for 12% -> 14% of each run, Pallas kernels for 0% -> 0%
where the time goes in v1:
time: 256 us; the launch traced here: 255 us
  waiting for transfers between devices  69.7 us (27%)
  local copies, waits for them, and re-layouts  47 us (18%)
  starting transfers between devices  36.1 us (14%)
  blocking collectives  32.9 us (13%)
  matrix products  32.6 us (13%)
  between operations  14.7 us (6%)
  loops' own time  11.8 us (5%)
  other arithmetic  10.6 us (4%)
    all_gather x1, waiting for transfers between devices, sent_together(): filled = lax.all_gather(both, axis, axis=dim, tiled=True)  52.2 us
    all_to_all x1, blocking collectives, sent_and_summed(): lax.all_to_all(tiles, axis, split_axis=0, concat_axis=0, tiled=True)  32.9 us
    dot_general x16, matrix products, attend_block(): jnp.einsum('qhd,khd->hqk', queries_h, keys_s, preferred_element_type=jnp....  18.9 us
    gather x10, local copies, waits for them, and re-layouts, per_device(): jnp.searchsorted(running, targets + 1)  18.9 us
    all_to_all x3, waiting for transfers between devices, copy_for_each(): return lax.all_to_all(copies, axis, split_axis=0, concat_axis=0, tiled=True)  17.5 us
    all_to_all x3, starting transfers between devices, copy_for_each(): return lax.all_to_all(copies, axis, split_axis=0, concat_axis=0, tiled=True)  16.9 us
    all_to_all x1, starting transfers between devices, choose_tracks_here(): top = all_to_all(formed, axis_id, 0, 0, tiled=True)  14.5 us
    another operation x1, loops' own time, per_device(): lax.scan(attend_block, running_state, jnp.arange(span_rows // query_rows,...  11.2 us
  transfers between devices with their start and end apart: 6, of which 3 were waited for; matrix products, arithmetic and copies ran while one was open for 14% of the time, Pallas kernels for 0%

profile of v1, /device:TPU:1, one launch (start us, length us, event | category | flops | bytes accessed | tf_op | source)
XLA Modules:
  0.0 255.2 jit_solution(12983609631383623301)
XLA Ops:
  6.5 4.6 %collective-permute-start = (s32[192]{0:T(256)}, s32[192]{0:T(256)S(1)}, u32[]{:S(2)}, u32[]{:S(2)}) collective-permute-start(s32[192]{0:T(256)} %param.14), channel_id=1, source_target_pairs={{0,4},{4,8},{8,12},{12,16},{16,20},{20,24},{24,28},{28,32},{32,36}... | collective-permute-start | bytes 2312 | tf_op jit(solution)/shard_map/ppermute | solution.py:19
  14.9 7.3 %all-to-all-start = ((s32[32,1,1]{2,1,0:T(1,128)}), s32[32,1,1]{2,1,0:T(1,128)S(1)}, u32[]{:S(2)}, u32[]{:S(2)}) async-start(s32[32,1,1]{2,1,0:T(1,128)} %broadcast_in_dim.111), calls=%async_computation | async-start | bytes 32768 | tf_op jit(solution)/shard_map/all_to_all | solution.py:24
  26.6 2.6 %all-to-all-done = s32[32,1,1]{2,1,0:T(1,128)S(1)} async-done(((s32[32,1,1]{2,1,0:T(1,128)}), s32[32,1,1]{2,1,0:T(1,128)S(1)}, u32[]{:S(2)}, u32[]{:S(2)}) %all-to-all-start) | async-done | bytes 160 | tf_op jit(solution)/shard_map/all_to_all | solution.py:24
  33.0 1.3 fusion.25
  37.2 4.8 %all-to-all-start.2 = ((bf16[32,72,256]{2,1,0:T(8,128)(2,1)}), bf16[32,72,256]{2,1,0:T(8,128)(2,1)S(1)}, u32[]{:S(2)}, u32[]{:S(2)}) async-start(bf16[32,72,256]{2,1,0:T(8,128)(2,1)} %broadcast_in_dim.118), calls=%async_computation.2 | async-start | bytes 2359296 | tf_op jit(solution)/shard_map/all_to_all | solution.py:24
  42.0 19.8 %while.39 = (s32[]{:T(128)}, u32[384]{0:T(512)S(1)}, u32[384]{0:T(512)S(1)}, s32[576]{0:T(1024)S(1)}, s32[]{:T(128)}, /*index=5*/s32[]{:T(128)}, s32[]{}) while((s32[]{:T(128)}, u32[384]{0:T(512)S(1)}, u32[384]{0:T(512)S(1)}, s32[576]{0:T(1024)S(1)}, s32[]{:T(128)}, /*index=5*/s32[]{:T(128)}, s32[]{}) %tuple.72), condition=%wide.region_10.11_spmd.clone, body=%wide.region_9.10_spmd.clone.sunk | while | flops 8324 | bytes 29541 | solution.py:155
  42.1 1.9 gather_fusion
  44.1 1.9 gather_fusion
  46.0 1.9 gather_fusion
  48.0 1.9 gather_fusion
  50.0 1.9 gather_fusion
  52.0 1.9 gather_fusion
  54.0 1.9 gather_fusion
  56.0 1.9 gather_fusion
  57.9 1.9 gather_fusion
  59.9 1.9 gather_fusion
  62.7 2.1 gather_fusion.2
  66.9 1.9 gather_fusion.1
  70.7 14.5 %all-to-all-start.1 = ((s32[16,384,1]{1,2,0:T(1,128)}), s32[16,384,1]{1,2,0:T(1,128)S(1)}, u32[]{:S(2)}, u32[]{:S(2)}) async-start(s32[16,384,1]{1,2,0:T(1,128)} %concatenate.15), calls=%async_computation.1 | async-start | bytes 49152 | tf_op jit(solution)/shard_map/all_to_all | solution.py:91
  85.7 52.2 %all-gather.2.cloned.1.call-done = bf16[6144,256]{0,1:T(8,128)(2,1)} async-done(((bf16[384,256]{0,1:T(8,128)(2,1)}), bf16[6144,256]{0,1:T(8,128)(2,1)}) %all-gather.2.cloned.1.call-update) | async-done | bytes 3145744 | tf_op jit(solution)/shard_map/all_gather | solution.py:41
  137.9 3.3 %fusion.52 = (bf16[6144,128]{0,1:T(8,128)(2,1)S(1)}, bf16[6144,128]{0,1:T(8,128)(2,1)}) fusion(bf16[6144,256]{0,1:T(8,128)(2,1)} %all-gather.2.cloned.1.call-done), kind=kLoop, calls=%fused_computation.120 | loop fusion | bytes 6291456 | tf_op jit(solution)/shard_map/split | solution.py:42
  141.1 49.5 %while.40 = (s32[]{:T(128)}, f32[1,384]{1,0:T(1,128)S(1)}, f32[1,384]{1,0:T(1,128)S(1)}, f32[384,1,128]{0,2,1:T(8,128)S(1)}, s32[16]{0:T(128)S(1)}, /*index=5*/s...) while((s32[]{:T(128)}, f32[1,384]{1,0:T(1,128)S(1)}, ...), condition=%wide.region_15.16_spmd.clone, body=%wide.region_12.15_spmd.clone.sunk | while | flops 77416712 | bytes 2498263 | solution.py:205
  142.5 1.2 fusion.84
  145.6 1.2 fusion.84
  148.7 1.2 fusion.84
  161.0 1.2 fusion.84
  164.1 1.2 fusion.84
  185.8 1.2 fusion.84
  188.9 1.2 fusion.84
  191.3 32.9 %all_to_all.30 = bf16[32,12,1024]{2,1,0:T(8,128)(2,1)S(1)} all-to-all(bf16[32,12,1024]{2,1,0:T(8,128)(2,1)S(1)} %reshape.271), channel_id=1, replica_groups=mesh['bytes'=16,'ctx'=8,'tp'=4] {'ctx','tp'}, dimensions={0} | all-to-all | bytes 1572864 | tf_op jit(solution)/shard_map/all_to_all | solution.py:52
  225.5 4.8 %all-to-all-start.4 = ((bf16[32,12,1024]{2,1,0:T(8,128)(2,1)}), bf16[32,12,1024]{2,1,0:T(8,128)(2,1)S(1)}, u32[]{:S(2)}, u32[]{:S(2)}) async-start(bf16[32,12,1024]{2,1,0:T(8,128)(2,1)} %broadcast_in_dim.119), calls=%async_computation.4 | async-start | bytes 2097152 | tf_op jit(solution)/shard_map/all_to_all | solution.py:24
  231.7 14.9 %all-to-all-done.4 = bf16[32,12,1024]{2,1,0:T(8,128)(2,1)S(1)} async-done(((bf16[32,12,1024]{2,1,0:T(8,128)(2,1)}), bf16[32,12,1024]{2,1,0:T(8,128)(2,1)S(1)}, u32[]{:S(2)}, u32[]{:S(2)}) %all-to-all-start.4) | async-done | bytes 786464 | tf_op jit(solution)/shard_map/all_to_all | solution.py:24
  (301 shorter events, 54.4 us)
Async XLA Ops:
  6.5 15.8 %copy-start = (bf16[256,1024]{1,0:T(8,128)(2,1)S(1)}, bf16[256,1024]{1,0:T(8,128)(2,1)}, u32[]{:S(2)}) copy-start(bf16[256,1024]{1,0:T(8,128)(2,1)} %param.16) | copy-start | bytes 1572868
  6.5 24.7 %collective-permute-start = (s32[192]{0:T(256)}, s32[192]{0:T(256)S(1)}, u32[]{:S(2)}, u32[]{:S(2)}) collective-permute-start(s32[192]{0:T(256)} %param.14), channel_id=1, source_target_pairs={{0,4},{4,8},{8,12},{12,16},{16,20},{20,24},{24,28},{28,32},{32,36}... | collective-permute-start | bytes 2312 | tf_op jit(solution)/shard_map/ppermute | solution.py:19
  12.5 0.6 copy-start.13
  13.1 10.4 %copy-start.17 = (s32[192]{0:T(256)}, s32[192]{0:T(256)S(1)}, u32[]{:S(2)}) copy-start(s32[192]{0:T(256)S(1)} %slice_add_fusion) | copy-start | bytes 2308
  14.9 14.2 %all-to-all-start = ((s32[32,1,1]{2,1,0:T(1,128)}), s32[32,1,1]{2,1,0:T(1,128)S(1)}, u32[]{:S(2)}, u32[]{:S(2)}) async-start(s32[32,1,1]{2,1,0:T(1,128)} %broadcast_in_dim.111), calls=%async_computation | async-start | bytes 32768 | tf_op jit(solution)/shard_map/all_to_all | solution.py:24
  22.3 1.3 copy-start.1
  23.5 1.0 copy-start.4
  23.7 1.1 copy-start.2
  26.4 5.8 %copy-start.6 = (pred[192,384]{1,0:T(8,128)(4,1)}, pred[192,384]{1,0:T(8,128)(4,1)S(1)}, u32[]{:S(2)}) copy-start(pred[192,384]{1,0:T(8,128)(4,1)S(1)} %fusion.34) | copy-start | bytes 221188
  26.6 5.7 %copy-start.3 = (bf16[192,256]{0,1:T(8,128)(2,1)}, bf16[192,256]{0,1:T(8,128)(2,1)S(1)}, u32[]{:S(2)}) copy-start(bf16[192,256]{0,1:T(8,128)(2,1)S(1)} %copy.33) | copy-start | bytes 294916
  30.0 0.6 copy-start.15
  31.7 0.6 copy-start.11
  33.0 1.4 copy-start.12
  33.0 1.7 copy-start.5
  34.4 0.9 copy-start.7
  35.2 0.6 copy-start.18
  35.2 0.6 copy-start.22
  35.8 1.4 copy-start.9
  37.2 24.7 %all-to-all-start.2 = ((bf16[32,72,256]{2,1,0:T(8,128)(2,1)}), bf16[32,72,256]{2,1,0:T(8,128)(2,1)S(1)}, u32[]{:S(2)}, u32[]{:S(2)}) async-start(bf16[32,72,256]{2,1,0:T(8,128)(2,1)} %broadcast_in_dim.118), calls=%async_computation.2 | async-start | bytes 2359296 | tf_op jit(solution)/shard_map/all_to_all | solution.py:24
  42.0 95.9 %all-gather.2.cloned.1.call-start = ((), (), s32[]{:S(2)}) async-start(), calls=%async_computation.5 | async-start | bytes 3342336 | tf_op jit(solution)/shard_map/all_gather | solution.py:41
  62.7 2.3 copy-start.19
  64.7 1.0 copy-start.20
  66.9 18.4 %copy-start.21 = (bf16[1024,128]{1,0:T(8,128)(2,1)S(1)}, bf16[1024,128]{1,0:T(8,128)(2,1)}, u32[]{:S(2)}) copy-start(bf16[1024,128]{1,0:T(8,128)(2,1)} %param.20) | copy-start | bytes 786436
  70.7 70.4 %all-to-all-start.1 = ((s32[16,384,1]{1,2,0:T(1,128)}), s32[16,384,1]{1,2,0:T(1,128)S(1)}, u32[]{:S(2)}, u32[]{:S(2)}) async-start(s32[16,384,1]{1,2,0:T(1,128)} %concatenate.15), calls=%async_computation.1 | async-start | bytes 49152 | tf_op jit(solution)/shard_map/all_to_all | solution.py:91
  141.1 49.5 %copy-start.8 = (bf16[128,1024]{1,0:T(8,128)(2,1)S(1)}, bf16[128,1024]{1,0:T(8,128)(2,1)}, u32[]{:S(2)}) copy-start(bf16[128,1024]{1,0:T(8,128)(2,1)} %param.23) | copy-start | bytes 786436
  225.5 4.8 %copy-start.16 = (s32[8]{0:T(128)S(1)}, s32[8]{0:T(128)}, u32[]{:S(2)}) copy-start(s32[8]{0:T(128)} %copy-done.15) | copy-start | bytes 100
  225.5 5.4 %copy-start.14 = (s32[256]{0:T(256)S(1)}, s32[256]{0:T(256)}, u32[]{:S(2)}) copy-start(s32[256]{0:T(256)} %copy-done.13) | copy-start | bytes 3076
  225.5 6.1 %copy-start.10 = (bf16[192,4,64]{0,2,1:T(8,128)(2,1)S(1)}, bf16[192,4,64]{0,2,1:T(8,128)(2,1)}, u32[]{:S(2)}) copy-start(bf16[192,4,64]{0,2,1:T(8,128)(2,1)} %copy-done.9) | copy-start | bytes 294916
  225.5 21.1 %all-to-all-start.4 = ((bf16[32,12,1024]{2,1,0:T(8,128)(2,1)}), bf16[32,12,1024]{2,1,0:T(8,128)(2,1)S(1)}, u32[]{:S(2)}, u32[]{:S(2)}) async-start(bf16[32,12,1024]{2,1,0:T(8,128)(2,1)} %broadcast_in_dim.119), calls=%async_computation.4 | async-start | bytes 2097152 | tf_op jit(solution)/shard_map/all_to_all | solution.py:24
Sparse Core Ops, SparseCore 0:
  67.0 70.7 all-gather.1
